TPU v7x, 32 devices: a whole 2x2x4 slice. The times are simulated.
32 devices in a mesh: tok: 8 (over y, x, core), slot: 4 (over z).
Axes of the slice: x: 2, y: 2, z: 4, core: 2. Of those that a mesh axis runs over, the one named last changes fastest.
Arguments:
- tokens: bfloat16 [8192, 1024], P('tok'), may hold values from -16 to 16
- slot_params: bfloat16 [8192, 1024], P('slot'), may hold values from -0.5 to 0.5
- w_in: bfloat16 [16, 1024, 4096], P('slot', None, 'tok'), may hold values from -0.1875 to 0.1875
- w_out: bfloat16 [16, 4096, 1024], P('slot', 'tok'), may hold values from -0.09375 to 0.09375
Outputs:
- mixed: bfloat16 [8192, 1024], P(('tok', 'slot'))
All inputs are finite; a program needn't handle non-finite values.
Results may differ from a plain program's by a relative error of at most 0.01.
Values may be sent and summed in bfloat16 or wider, within the bound.
No kernel may reach another device: no remote copies, remote signals or barrier semaphores. Data moves between devices by JAX's collectives and lax.ppermute only.
A program may use at most 64 MiB of HBM per device.

v0:
```python
import jax
import jax.numpy as jnp
from jax import lax
from jax.sharding import PartitionSpec as P

P_SIZE = 8


def body(tokens, slot_params, w_in, w_out):
    experts_here = w_in.shape[0]
    in_flight = experts_here * P_SIZE
    logits = lax.dot_general(
        slot_params, tokens, (((1,), (1,)), ((), ())), preferred_element_type=jnp.float32
    )
    flight = logits[:in_flight]
    col_max = lax.pmax(jnp.max(flight, axis=1), "tok")
    dispatch_exp = jnp.exp(flight - col_max[:, None])
    dispatch_w = dispatch_exp.astype(jnp.bfloat16)
    numer = jnp.dot(dispatch_w, tokens, preferred_element_type=jnp.float32)
    numer, totals = lax.psum((numer, jnp.sum(dispatch_exp, axis=1)), "tok")
    slot_in = (
        (numer / totals[:, None]).astype(jnp.bfloat16).reshape(experts_here, P_SIZE, numer.shape[1])
    )
    pre_act = jnp.einsum("epd,edh->eph", slot_in, w_in, preferred_element_type=jnp.float32)
    hidden = jax.nn.gelu(pre_act).astype(jnp.bfloat16)
    partial_out = jnp.einsum("eph,ehd->epd", hidden, w_out, preferred_element_type=jnp.float32)
    partial_out = partial_out.reshape(in_flight, partial_out.shape[2])
    slot_out = lax.psum(partial_out, "tok").astype(jnp.bfloat16)
    row_max = lax.pmax(jnp.max(logits, axis=0), "slot")
    row_sum = lax.psum(jnp.sum(jnp.exp(logits - row_max[None, :]), axis=0), "slot")
    combine_w = (jnp.exp(flight - row_max[None, :]) / row_sum[None, :]).astype(jnp.bfloat16)
    token_weights = lax.all_to_all(combine_w, "slot", split_axis=1, concat_axis=0, tiled=True)
    all_outputs = lax.all_gather(slot_out, "slot", axis=0, tiled=True)
    mixed = lax.dot_general(
        token_weights, all_outputs, (((0,), (0,)), ((), ())), preferred_element_type=jnp.float32
    )
    return mixed.astype(jnp.bfloat16)


def solution(mesh):
    return jax.shard_map(
        body,
        mesh=mesh,
        in_specs=(P("tok", None), P("slot", None), P("slot", None, "tok"), P("slot", "tok", None)),
        out_specs=P(("tok", "slot"), None),
        check_vma=False,
    )
```

profile of v0, /device:TPU:0, one launch (start us, length us, event | category | flops | bytes accessed | tf_op | source)
XLA Modules:
  0.0 138.5 jit_solution(10838787701703055438)
XLA Ops:
  6.5 0.0 copy-start
  6.5 0.0 all-reduce.3.cloned.1.call-start
  6.5 1.6 %copy-done = bf16[1024,1024]{1,0:T(8,128)(2,1)S(1)} copy-done((bf16[1024,1024]{1,0:T(8,128)(2,1)S(1)}, bf16[1024,1024]{1,0:T(8,128)(2,1)}, u32[]{:S(2)}) %copy-start) | copy-done | bytes 2097176
  8.1 6.4 %fusion.27 = (f32[1024]{0:T(1024)S(1)}, f32[2048,1024]{1,0:T(8,128)S(1)}) fusion(bf16[2048,1024]{1,0:T(8,128)(2,1)} %param.5, bf16[1024,1024]{1,0:T(8,128)(2,1)S(1)} %copy-done), kind=kOutput, calls=%fused_computation.31 | convolution fusion | flops 4297063424 | bytes 14684160 | tf_op jit(solution)/shard_map/dot_general | solution.py:12
  14.5 0.0 copy-start.1
  14.5 3.2 %copy-done.1 = f32[2048,1024]{1,0:T(8,128)} copy-done((f32[2048,1024]{1,0:T(8,128)}, f32[2048,1024]{1,0:T(8,128)S(1)}, u32[]{:S(2)}) %copy-start.1) | copy-done | bytes 8388632
  17.7 0.1 slice_reduce_fusion
  17.8 15.2 %pmax.15 = f32[32]{0:T(128)S(1)} all-reduce(f32[32]{0:T(128)S(1)} %slice_reduce_fusion), channel_id=1, replica_groups=mesh['tok'=8,'slot'=4] {'tok'}, use_global_device_ids=true, to_apply=%region_5.0 | all-reduce | flops 32 | bytes 256 | tf_op jit(solution)/shard_map/pmax | solution.py:16
  33.0 2.1 %fusion.10 = f32[32,1024]{1,0:T(8,128)} fusion(bf16[1024,1024]{1,0:T(8,128)(2,1)S(1)} %copy-done, f32[2048,1024]{1,0:T(8,128)} %copy-done.1, f32[32]{0:T(128)S(1)} %pmax.15), kind=kOutput, calls=%fused_computation.18 | convolution fusion | flops 67174400 | bytes 2359424 | tf_op jit(solution)/shard_map/dot_general | solution.py:19
  35.1 0.0 all-reduce.3.cloned.1.call-update
  35.1 12.0 %pmax.14 = f32[1024]{0:T(1024)S(1)} all-reduce(f32[1024]{0:T(1024)S(1)} %get-tuple-element.7), channel_id=1, replica_groups=mesh['tok'=8,'slot'=4] {'slot'}, use_global_device_ids=true, to_apply=%region_1.0 | all-reduce | flops 1024 | bytes 8192 | tf_op jit(solution)/shard_map/pmax | solution.py:29
  47.1 4.6 %exponential_reduce_fusion = f32[1024]{0:T(1024)S(1)} fusion(f32[2048,1024]{1,0:T(8,128)} %copy-done.1, f32[1024]{0:T(1024)S(1)} %pmax.14), kind=kLoop, calls=%fused_computation | loop fusion | flops 4193280 | bytes 8396800 | tf_op jit(solution)/shard_map/reduce_sum | solution.py:30
  51.6 8.4 %psum.28 = f32[1024]{0:T(1024)S(1)} all-reduce(f32[1024]{0:T(1024)S(1)} %exponential_reduce_fusion), channel_id=1, replica_groups=mesh['tok'=8,'slot'=4] {'slot'}, use_global_device_ids=true, to_apply=%region_3.0 | all-reduce | flops 1024 | bytes 8192 | tf_op jit(solution)/shard_map/psum | solution.py:30
  60.0 1.1 fusion
  61.1 0.6 copy.8
  61.8 3.3 %all-to-all-start = ((bf16[32,4,256]{2,0,1:T(8,128)(2,1)}), bf16[32,4,256]{2,0,1:T(8,128)(2,1)S(1)}, u32[]{:S(2)}, u32[]{:S(2)}) async-start(bf16[32,4,256]{2,0,1:T(8,128)(2,1)} %bitcast.22), calls=%async_computation | async-start | bytes 131072 | tf_op jit(solution)/shard_map/all_to_all | solution.py:32
  65.0 11.9 %psum.30 = f32[32]{0:T(128)S(1)} all-reduce(f32[32]{0:T(128)S(1)} %get-tuple-element.5), channel_id=1, replica_groups=mesh['tok'=8,'slot'=4] {'tok'}, use_global_device_ids=true, to_apply=%region_8.0 | all-reduce | flops 32 | bytes 256 | tf_op jit(solution)/shard_map/psum | solution.py:20
  76.9 11.1 %all-reduce.3.cloned.1.call-done = f32[32,1024]{1,0:T(8,128)} async-done(((f32[32,1024]{1,0:T(8,128)}), f32[32,1024]{1,0:T(8,128)}) %all-reduce.3.cloned.1.call-update) | async-done | bytes 131088 | tf_op jit(solution)/shard_map/psum | solution.py:20
  88.1 4.7 %convolution_bitcast_fusion = f32[32,1024]{1,0:T(8,128)S(1)} fusion(bf16[4,512,1024]{2,1,0:T(8,128)(2,1)} %param.7, bf16[4,1024,512]{2,1,0:T(8,128)(2,1)} %param.6, f32[32,1024]{1,0:T(8,128)} %all-reduce.3.cloned.1.call-done, f32[32]{0:T(128)S(1)} %psum.30), kind=kOutput, calls=%fused_computation.2 | convolution fusion | flops 67321856 | bytes 8650880 | tf_op jit(solution)/shard_map/eph,ehd->epd/dot_general | solution.py:26
  92.8 23.4 %all-reduce.4 = bf16[32,1024]{1,0:T(8,128)(2,1)S(1)} all-reduce(f32[32,1024]{1,0:T(8,128)S(1)} %convolution_bitcast_fusion), channel_id=1, replica_groups=mesh['tok'=8,'slot'=4] {'tok'}, use_global_device_ids=true, to_apply=%region_9.0 | all-reduce | flops 32768 | bytes 196608 | tf_op jit(solution)/shard_map/psum | solution.py:28
  116.3 14.3 %all_gather.3 = bf16[128,1024]{1,0:T(8,128)(2,1)S(1)} all-gather(bf16[32,1024]{1,0:T(8,128)(2,1)S(1)} %all-reduce.4), channel_id=1, replica_groups=mesh['tok'=8,'slot'=4] {'slot'}, dimensions={0}, use_global_device_ids=true | all-gather | bytes 327680 | tf_op jit(solution)/shard_map/all_gather | solution.py:33
  130.6 0.0 all-to-all-done
  130.6 1.1 convolution_convert_fusion
Async XLA Ops:
  6.5 1.6 %copy-start = (bf16[1024,1024]{1,0:T(8,128)(2,1)S(1)}, bf16[1024,1024]{1,0:T(8,128)(2,1)}, u32[]{:S(2)}) copy-start(bf16[1024,1024]{1,0:T(8,128)(2,1)} %param.4) | copy-start | bytes 6291460
  6.5 81.5 %all-reduce.3.cloned.1.call-start = ((), (), s32[]{:S(2)}) async-start(), calls=%async_computation.1 | async-start | bytes 262144 | tf_op jit(solution)/shard_map/psum | solution.py:20
  14.5 3.2 %copy-start.1 = (f32[2048,1024]{1,0:T(8,128)}, f32[2048,1024]{1,0:T(8,128)S(1)}, u32[]{:S(2)}) copy-start(f32[2048,1024]{1,0:T(8,128)S(1)} %get-tuple-element.8) | copy-start | bytes 25165828
  61.8 68.8 %all-to-all-start = ((bf16[32,4,256]{2,0,1:T(8,128)(2,1)}), bf16[32,4,256]{2,0,1:T(8,128)(2,1)S(1)}, u32[]{:S(2)}, u32[]{:S(2)}) async-start(bf16[32,4,256]{2,0,1:T(8,128)(2,1)} %bitcast.22), calls=%async_computation | async-start | bytes 131072 | tf_op jit(solution)/shard_map/all_to_all | solution.py:32
Sparse Core Ops, SparseCore 0:
  35.2 52.7 all-reduce.2
where the time goes:
time: 139 us
  blocking collectives  85.1 us (61%)
  matrix products  14.3 us (10%)
  between operations  13.4 us (10%)
  waiting for transfers between devices  11.1 us (8%)
  other arithmetic  5.79 us (4%)
  local copies, waits for them, and re-layouts  5.43 us (4%)
  starting transfers between devices  3.29 us (2%)
    psum x1, blocking collectives, body(): slot_out = lax.psum(partial_out, 'tok').astype(jnp.bfloat16)  23.4 us
    pmax x1, blocking collectives, body(): col_max = lax.pmax(jnp.max(flight, axis=1), 'tok')  15.2 us
    all_gather x1, blocking collectives, body(): all_outputs = lax.all_gather(slot_out, 'slot', axis=0, tiled=True)  14.3 us
    pmax x1, blocking collectives, body(): row_max = lax.pmax(jnp.max(logits, axis=0), 'slot')  12 us
    psum x1, blocking collectives, body(): numer, totals = lax.psum((numer, jnp.sum(dispatch_exp, axis=1)), 'tok')  11.9 us
    psum x1, waiting for transfers between devices, body(): numer, totals = lax.psum((numer, jnp.sum(dispatch_exp, axis=1)), 'tok')  11.1 us
    psum x1, blocking collectives, body(): lax.psum(jnp.sum(jnp.exp(logits - row_max[None, :]), axis=0), 'slot')  8.37 us
    dot_general x1, matrix products, body(): lax.dot_general(slot_params, tokens, (((1,), (1,)), ((), ())), preferred_...  6.38 us
  transfers between devices with their start and end apart: 2, of which 1 were waited for; matrix products, arithmetic and copies ran while one was open for 8% of the time, Pallas kernels for 0%

commit v1 on v0

--- a/solution.py
+++ b/solution.py
@@ -27,7 +27,9 @@
     partial_out = partial_out.reshape(in_flight, partial_out.shape[2])
     slot_out = lax.psum(partial_out, "tok").astype(jnp.bfloat16)
     row_max = lax.pmax(jnp.max(logits, axis=0), "slot")
-    row_sum = lax.psum(jnp.sum(jnp.exp(logits - row_max[None, :]), axis=0), "slot")
+    row_sum = jnp.sum(
+        lax.all_gather(jnp.sum(jnp.exp(logits - row_max[None, :]), axis=0), "slot"), axis=0
+    )
     combine_w = (jnp.exp(flight - row_max[None, :]) / row_sum[None, :]).astype(jnp.bfloat16)
     token_weights = lax.all_to_all(combine_w, "slot", split_axis=1, concat_axis=0, tiled=True)
     all_outputs = lax.all_gather(slot_out, "slot", axis=0, tiled=True)

time: 139 us -> 139 us (level)
  blocking collectives: 85.1 us -> 89.9 us
  waiting for transfers between devices: 11.1 us -> 6.36 us
    all_gather x0 -> x1, blocking collectives: none -> 13.2 us  [body(): lax.all_gather(jnp.sum(jnp.exp(logits - row_max[None, :]), axis=0), 'slot')]
    psum x1 -> x0, blocking collectives: 8.37 us -> none  [body(): lax.psum(jnp.sum(jnp.exp(logits - row_max[None, :]), axis=0), 'slot')]
    psum x1, waiting for transfers between devices: 11.1 us -> 6.34 us  [body(): numer, totals = lax.psum((numer, jnp.sum(dispatch_exp, axis=1)), 'tok')]
where the time goes in v1:
time: 139 us
  blocking collectives  89.9 us (65%)
  matrix products  14.3 us (10%)
  between operations  13.4 us (10%)
  waiting for transfers between devices  6.36 us (5%)
  other arithmetic  5.81 us (4%)
  local copies, waits for them, and re-layouts  5.44 us (4%)
  starting transfers between devices  3.28 us (2%)
    psum x1, blocking collectives, body(): slot_out = lax.psum(partial_out, 'tok').astype(jnp.bfloat16)  23.4 us
    pmax x1, blocking collectives, body(): col_max = lax.pmax(jnp.max(flight, axis=1), 'tok')  15.2 us
    all_gather x1, blocking collectives, body(): all_outputs = lax.all_gather(slot_out, 'slot', axis=0, tiled=True)  14.3 us
    all_gather x1, blocking collectives, body(): lax.all_gather(jnp.sum(jnp.exp(logits - row_max[None, :]), axis=0), 'slot')  13.2 us
    pmax x1, blocking collectives, body(): row_max = lax.pmax(jnp.max(logits, axis=0), 'slot')  12 us
    psum x1, blocking collectives, body(): numer, totals = lax.psum((numer, jnp.sum(dispatch_exp, axis=1)), 'tok')  11.8 us
    dot_general x1, matrix products, body(): lax.dot_general(slot_params, tokens, (((1,), (1,)), ((), ())), preferred_...  6.37 us
    psum x1, waiting for transfers between devices, body(): numer, totals = lax.psum((numer, jnp.sum(dispatch_exp, axis=1)), 'tok')  6.34 us
  transfers between devices with their start and end apart: 2, of which 1 were waited for; matrix products, arithmetic and copies ran while one was open for 8% of the time, Pallas kernels for 0%

profile of v1, /device:TPU:0, one launch (start us, length us, event | category | flops | bytes accessed | tf_op | source)
XLA Modules:
  0.0 138.5 jit_solution(13865976925181170559)
XLA Ops:
  6.5 0.0 copy-start
  6.5 0.0 all-reduce.3.cloned.1.call-start
  6.5 1.6 %copy-done = bf16[1024,1024]{1,0:T(8,128)(2,1)S(1)} copy-done((bf16[1024,1024]{1,0:T(8,128)(2,1)S(1)}, bf16[1024,1024]{1,0:T(8,128)(2,1)}, u32[]{:S(2)}) %copy-start) | copy-done | bytes 2097176
  8.1 6.4 %fusion.27 = (f32[1024]{0:T(1024)S(1)}, f32[2048,1024]{1,0:T(8,128)S(1)}) fusion(bf16[2048,1024]{1,0:T(8,128)(2,1)} %param.5, bf16[1024,1024]{1,0:T(8,128)(2,1)S(1)} %copy-done), kind=kOutput, calls=%fused_computation.31 | convolution fusion | flops 4297063424 | bytes 14684160 | tf_op jit(solution)/shard_map/dot_general | solution.py:12
  14.5 0.0 copy-start.1
  14.5 3.2 %copy-done.1 = f32[2048,1024]{1,0:T(8,128)} copy-done((f32[2048,1024]{1,0:T(8,128)}, f32[2048,1024]{1,0:T(8,128)S(1)}, u32[]{:S(2)}) %copy-start.1) | copy-done | bytes 8388632
  17.7 0.1 slice_reduce_fusion
  17.8 15.2 %pmax.15 = f32[32]{0:T(128)S(1)} all-reduce(f32[32]{0:T(128)S(1)} %slice_reduce_fusion), channel_id=1, replica_groups=mesh['tok'=8,'slot'=4] {'tok'}, use_global_device_ids=true, to_apply=%region_5.0 | all-reduce | flops 32 | bytes 256 | tf_op jit(solution)/shard_map/pmax | solution.py:16
  33.0 2.1 %fusion.10 = f32[32,1024]{1,0:T(8,128)} fusion(bf16[1024,1024]{1,0:T(8,128)(2,1)S(1)} %copy-done, f32[2048,1024]{1,0:T(8,128)} %copy-done.1, f32[32]{0:T(128)S(1)} %pmax.15), kind=kOutput, calls=%fused_computation.18 | convolution fusion | flops 67174400 | bytes 2359424 | tf_op jit(solution)/shard_map/dot_general | solution.py:19
  35.1 0.0 all-reduce.3.cloned.1.call-update
  35.1 12.0 %pmax.14 = f32[1024]{0:T(1024)S(1)} all-reduce(f32[1024]{0:T(1024)S(1)} %get-tuple-element.7), channel_id=1, replica_groups=mesh['tok'=8,'slot'=4] {'slot'}, use_global_device_ids=true, to_apply=%region_1.0 | all-reduce | flops 1024 | bytes 8192 | tf_op jit(solution)/shard_map/pmax | solution.py:29
  47.1 4.6 %exponential_reduce_fusion = f32[1024]{0:T(1024)S(1)} fusion(f32[2048,1024]{1,0:T(8,128)} %copy-done.1, f32[1024]{0:T(1024)S(1)} %pmax.14), kind=kLoop, calls=%fused_computation | loop fusion | flops 4193280 | bytes 8396800 | tf_op jit(solution)/shard_map/reduce_sum | solution.py:31
  51.6 13.2 %all-gather = f32[4096]{0:T(1024)S(1)} all-gather(f32[1024]{0:T(1024)S(1)} %exponential_reduce_fusion), channel_id=2, replica_groups=mesh['tok'=8,'slot'=4] {'slot'}, dimensions={0}, use_global_device_ids=true | all-gather | bytes 20480 | tf_op jit(solution)/shard_map/all_gather | solution.py:31
  64.9 1.1 fusion
  66.0 0.6 copy.10
  66.6 3.3 %all-to-all-start = ((bf16[32,4,256]{2,0,1:T(8,128)(2,1)}), bf16[32,4,256]{2,0,1:T(8,128)(2,1)S(1)}, u32[]{:S(2)}, u32[]{:S(2)}) async-start(bf16[32,4,256]{2,0,1:T(8,128)(2,1)} %bitcast.22), calls=%async_computation | async-start | bytes 131072 | tf_op jit(solution)/shard_map/all_to_all | solution.py:34
  69.9 11.8 %psum.22 = f32[32]{0:T(128)S(1)} all-reduce(f32[32]{0:T(128)S(1)} %get-tuple-element.5), channel_id=1, replica_groups=mesh['tok'=8,'slot'=4] {'tok'}, use_global_device_ids=true, to_apply=%region_8.0 | all-reduce | flops 32 | bytes 256 | tf_op jit(solution)/shard_map/psum | solution.py:20
  81.7 6.3 %all-reduce.3.cloned.1.call-done = f32[32,1024]{1,0:T(8,128)} async-done(((f32[32,1024]{1,0:T(8,128)}), f32[32,1024]{1,0:T(8,128)}) %all-reduce.3.cloned.1.call-update) | async-done | bytes 131088 | tf_op jit(solution)/shard_map/psum | solution.py:20
  88.1 4.7 %convolution_bitcast_fusion = f32[32,1024]{1,0:T(8,128)S(1)} fusion(bf16[4,512,1024]{2,1,0:T(8,128)(2,1)} %param.7, bf16[4,1024,512]{2,1,0:T(8,128)(2,1)} %param.6, f32[32,1024]{1,0:T(8,128)} %all-reduce.3.cloned.1.call-done, f32[32]{0:T(128)S(1)} %psum.22), kind=kOutput, calls=%fused_computation.2 | convolution fusion | flops 67321856 | bytes 8650880 | tf_op jit(solution)/shard_map/eph,ehd->epd/dot_general | solution.py:26
  92.8 23.4 %all-reduce.4 = bf16[32,1024]{1,0:T(8,128)(2,1)S(1)} all-reduce(f32[32,1024]{1,0:T(8,128)S(1)} %convolution_bitcast_fusion), channel_id=1, replica_groups=mesh['tok'=8,'slot'=4] {'tok'}, use_global_device_ids=true, to_apply=%region_9.0 | all-reduce | flops 32768 | bytes 196608 | tf_op jit(solution)/shard_map/psum | solution.py:28
  116.3 14.3 %all_gather.11 = bf16[128,1024]{1,0:T(8,128)(2,1)S(1)} all-gather(bf16[32,1024]{1,0:T(8,128)(2,1)S(1)} %all-reduce.4), channel_id=1, replica_groups=mesh['tok'=8,'slot'=4] {'slot'}, dimensions={0}, use_global_device_ids=true | all-gather | bytes 327680 | tf_op jit(solution)/shard_map/all_gather | solution.py:35
  130.6 0.0 all-to-all-done
  130.6 1.1 convolution_convert_fusion
  (2 shorter events, 0.0 us)
Async XLA Ops:
  6.5 1.6 %copy-start = (bf16[1024,1024]{1,0:T(8,128)(2,1)S(1)}, bf16[1024,1024]{1,0:T(8,128)(2,1)}, u32[]{:S(2)}) copy-start(bf16[1024,1024]{1,0:T(8,128)(2,1)} %param.4) | copy-start | bytes 6291460
  6.5 81.5 %all-reduce.3.cloned.1.call-start = ((), (), s32[]{:S(2)}) async-start(), calls=%async_computation.1 | async-start | bytes 262144 | tf_op jit(solution)/shard_map/psum | solution.py:20
  14.5 3.2 %copy-start.1 = (f32[2048,1024]{1,0:T(8,128)}, f32[2048,1024]{1,0:T(8,128)S(1)}, u32[]{:S(2)}) copy-start(f32[2048,1024]{1,0:T(8,128)S(1)} %get-tuple-element.8) | copy-start | bytes 25165828
  66.6 63.9 %all-to-all-start = ((bf16[32,4,256]{2,0,1:T(8,128)(2,1)}), bf16[32,4,256]{2,0,1:T(8,128)(2,1)S(1)}, u32[]{:S(2)}, u32[]{:S(2)}) async-start(bf16[32,4,256]{2,0,1:T(8,128)(2,1)} %bitcast.22), calls=%async_computation | async-start | bytes 131072 | tf_op jit(solution)/shard_map/all_to_all | solution.py:34
Sparse Core Ops, SparseCore 0:
  35.2 52.7 all-reduce.2
